TPU v7x, 32 devices: a whole 2x2x4 slice. The times are simulated.
32 devices in a mesh: seq: 8 (over z, x), tp: 4 (over y, core).
Axes of the slice: x: 2, y: 2, z: 4, core: 2. Of those that a mesh axis runs over, the one named last changes fastest.
Arguments:
- inputs: bfloat16 [2, 2048, 2048], P(None, 'seq'), may hold values from -6 to 6
- cotangent: bfloat16 [2, 2048, 2048], P(None, 'seq'), may hold values from -6 to 6
- attn_gain: bfloat16 [2048], P('seq'), may hold values from 0.5 to 1.5
- w_query: bfloat16 [2048, 2048], P('seq', 'tp'), may hold values from -0.125 to 0.125
- w_key: bfloat16 [2048, 2048], P('seq', 'tp'), may hold values from -0.125 to 0.125
- w_value: bfloat16 [2048, 3456], P('seq', 'tp'), may hold values from -0.125 to 0.125
- w_gate: bfloat16 [2048, 3456], P('seq', 'tp'), may hold values from -0.125 to 0.125
- w_out: bfloat16 [3456, 2048], P('tp', 'seq'), may hold values from -0.15625 to 0.15625
- ffn_gain: bfloat16 [2048], P('seq'), may hold values from 0.5 to 1.5
- w_glu: bfloat16 [2048, 3456], P('seq', 'tp'), may hold values from -0.125 to 0.125
- w_up: bfloat16 [2048, 3456], P('seq', 'tp'), may hold values from -0.125 to 0.125
- w_down: bfloat16 [3456, 2048], P('tp', 'seq'), may hold values from -0.15625 to 0.15625
- decay_rate: float32 [8], P('tp'), may hold values from 0 to 0.032, as said below
Outputs:
- outputs: bfloat16 [2, 2048, 2048], P(None, 'seq')
- input_grad: float32 [2, 2048, 2048], P(None, 'seq')
- attngain_grad: float32 [2048], P('seq')
- query_grad: float32 [2048, 2048], P('seq', 'tp')
- key_grad: float32 [2048, 2048], P('seq', 'tp')
- value_grad: float32 [2048, 3456], P('seq', 'tp')
- gate_grad: float32 [2048, 3456], P('seq', 'tp')
- out_grad: float32 [3456, 2048], P('tp', 'seq')
- ffngain_grad: float32 [2048], P('seq')
- glu_grad: float32 [2048, 3456], P('seq', 'tp')
- up_grad: float32 [2048, 3456], P('seq', 'tp')
- down_grad: float32 [3456, 2048], P('tp', 'seq')
Inputs may be any that keep to these rules, and one draw needn't show every extreme that they name: `decay_rate`: each head's decay rate; positive.
All inputs are finite; a program needn't handle non-finite values.
Results may differ from a plain program's by a relative error of at most 0.03.
Values may be sent and summed in bfloat16 or wider, within the bound.
A program may use at most 256 MiB of HBM per device.

v0:
```python
import math
import jax
import jax.numpy as jnp
from jax import lax
from jax.sharding import PartitionSpec as P

KEY = 256
VAL = 432
EPS_LAYER = 1e-05
EPS_GROUP = 1e-06
MAXIMAL_ACCURACY = lax.Precision.HIGHEST


def passed_along(block, axis, distance):
    devices = range(lax.axis_size(axis))
    route = [(i - distance, i) for i in devices if i - distance in devices]
    return lax.ppermute(block, axis, route)


def normalize(values, epsilon):
    average = jnp.mean(values, axis=-1, keepdims=True)
    centred = values - average
    inv_std = lax.rsqrt(jnp.mean(centred * centred, axis=-1, keepdims=True) + epsilon)
    return (centred * inv_std, inv_std)


def normalize_back(upstream, normed, inv_std):
    return inv_std * (
        upstream
        - jnp.mean(upstream, axis=-1, keepdims=True)
        - normed * jnp.mean(upstream * normed, axis=-1, keepdims=True)
    )


def swish_parts(values):
    sigmoid = jax.nn.sigmoid(values)
    return (values * sigmoid, sigmoid * (1.0 + values * (1.0 - sigmoid)))


def rotary_tables(positions, width):
    half_width = width // 2
    fraction = jnp.arange(half_width, dtype=jnp.float32) / max(half_width - 1, 1)
    frequency = jnp.power(10000.0, -fraction)
    angles = positions[:, None] * frequency[None, :]
    cosine = jnp.concatenate([jnp.cos(angles), jnp.cos(angles)], axis=-1)[:, None, :]
    sine_table = jnp.concatenate([jnp.sin(angles), jnp.sin(angles)], axis=-1)[:, None, :]
    return (cosine, sine_table)


def rotate(values, cosine, sine_table):
    half_width = values.shape[-1] // 2
    turned = jnp.concatenate([-values[..., half_width:], values[..., :half_width]], axis=-1)
    return values * cosine + turned * sine_table


def rotate_back(upstream, cosine, sine_table):
    half_width = upstream.shape[-1] // 2
    scaled = upstream * sine_table
    turned = jnp.concatenate([scaled[..., half_width:], -scaled[..., :half_width]], axis=-1)
    return upstream * cosine + turned


def decay_tables(rates, length):
    offsets = jnp.arange(length, dtype=jnp.float32)
    distance = offsets[:, None] - offsets[None, :]
    decay_mask = jnp.where(
        distance[None] >= 0.0,
        jnp.exp(-rates[:, None, None] * jnp.maximum(distance, 0.0)[None]),
        0.0,
    )
    leading_decay = jnp.exp(-rates[None, :] * (offsets[:, None] + 1.0))
    trailing_decay = jnp.exp(-rates[None, :] * (length - 1.0 - offsets[:, None]))
    return (decay_mask, leading_decay, trailing_decay)


def block_summary(key_rotated, value_matrix_rows, trailing_decay):
    return jnp.einsum(
        "ysu,ysb->sub",
        key_rotated.astype(jnp.float32) * trailing_decay[:, :, None],
        value_matrix_rows.astype(jnp.float32),
        precision=MAXIMAL_ACCURACY,
    )


def block_weights(query_rotated, key_rotated, decay_mask):
    scores = jnp.einsum(
        "ihk,jhk->hij", query_rotated, key_rotated, preferred_element_type=jnp.float32
    )
    return (scores * decay_mask).astype(jnp.bfloat16)


def block_output(
    query_rotated, key_rotated, value_matrix_rows, incoming_state, decay_mask, leading_decay
):
    layer_weights = block_weights(query_rotated, key_rotated, decay_mask)
    inner = jnp.einsum(
        "hij,jhv->ihv", layer_weights, value_matrix_rows, preferred_element_type=jnp.float32
    )
    carried_state = jnp.einsum(
        "jnq,nqs->jns",
        query_rotated.astype(jnp.float32) * leading_decay[:, :, None],
        incoming_state,
        precision=MAXIMAL_ACCURACY,
    )
    return inner + carried_state


def state_grad_own(query_rotated, output_gradient, leading_decay):
    return jnp.einsum(
        "pxa,pxb->xab",
        query_rotated.astype(jnp.float32) * leading_decay[:, :, None],
        output_gradient.astype(jnp.float32),
        precision=MAXIMAL_ACCURACY,
    )


def block_backward(
    query_rotated,
    key_rotated,
    value_matrix_rows,
    incoming_state,
    state_gradient,
    output_gradient,
    decay_mask,
    leading_decay,
    trailing_decay,
):
    weight_gradients = (
        jnp.einsum(
            "ihv,jhv->hij", output_gradient, value_matrix_rows, preferred_element_type=jnp.float32
        )
        * decay_mask
    ).astype(jnp.bfloat16)
    layer_weights = block_weights(query_rotated, key_rotated, decay_mask)
    query_gradient = jnp.einsum(
        "pzg,gpe->zpe", weight_gradients, key_rotated, preferred_element_type=jnp.float32
    ) + leading_decay[:, :, None] * jnp.einsum(
        "wcr,cdr->wcd",
        output_gradient.astype(jnp.float32),
        incoming_state,
        precision=MAXIMAL_ACCURACY,
    )
    key_gradient = jnp.einsum(
        "zun,uzf->nzf", weight_gradients, query_rotated, preferred_element_type=jnp.float32
    ) + trailing_decay[:, :, None] * jnp.einsum(
        "crp,rnp->crn",
        value_matrix_rows.astype(jnp.float32),
        state_gradient,
        precision=MAXIMAL_ACCURACY,
    )
    value_gradient = jnp.einsum(
        "lpb,plz->blz", layer_weights, output_gradient, preferred_element_type=jnp.float32
    ) + trailing_decay[:, :, None] * jnp.einsum(
        "zmf,mfn->zmn", key_rotated.astype(jnp.float32), state_gradient, precision=MAXIMAL_ACCURACY
    )
    return (query_gradient, key_gradient, value_gradient)


def carry_states(whole_decay, summary):

    def advance(turn_index, carried_state):
        return passed_along(whole_decay * carried_state + summary, "seq", 1)

    return lax.fori_loop(0, lax.axis_size("seq") - 1, advance, jnp.zeros_like(summary))


def carry_back(whole_decay, own_grad):

    def retreat(turn_index, carried_state):
        return passed_along(whole_decay * carried_state + own_grad, "seq", -1)

    return lax.fori_loop(0, lax.axis_size("seq") - 1, retreat, jnp.zeros_like(own_grad))


def on_device(
    inputs,
    cotangent,
    attn_gain,
    w_query,
    w_key,
    w_value,
    w_gate,
    w_out,
    ffn_gain,
    w_glu,
    w_up,
    w_down,
    decay_rate,
):
    seq_count, tok_rows, model_width = inputs.shape
    row_count = seq_count * tok_rows
    local_heads = decay_rate.shape[0]
    gathered = (
        lax.all_gather(w_query, "seq", axis=0, tiled=True),
        lax.all_gather(w_key, "seq", axis=0, tiled=True),
        lax.all_gather(w_value, "seq", axis=0, tiled=True),
        lax.all_gather(w_gate, "seq", axis=0, tiled=True),
        lax.all_gather(w_out, "seq", axis=1, tiled=True),
        lax.all_gather(w_glu, "seq", axis=0, tiled=True),
        lax.all_gather(w_up, "seq", axis=0, tiled=True),
        lax.all_gather(w_down, "seq", axis=1, tiled=True),
        lax.all_gather(attn_gain, "seq", axis=0, tiled=True),
        lax.all_gather(ffn_gain, "seq", axis=0, tiled=True),
    )
    (
        full_query,
        full_key,
        full_value,
        full_gate,
        full_out,
        full_glu,
        full_up,
        full_down,
        full_attn_gain,
        full_ffn_gain,
    ) = gathered
    residual = inputs.astype(jnp.float32).reshape(row_count, model_width)
    normed_one, inv_one = normalize(residual, EPS_LAYER)
    attn_in = (normed_one * full_attn_gain.astype(jnp.float32)).astype(jnp.bfloat16)
    query_lin = jnp.dot(attn_in, full_query, preferred_element_type=jnp.float32)
    key_lin = jnp.dot(attn_in, full_key, preferred_element_type=jnp.float32)
    value_lin = jnp.dot(attn_in, full_value, preferred_element_type=jnp.float32)
    gate_lin = jnp.dot(attn_in, full_gate, preferred_element_type=jnp.float32)
    offset = (lax.axis_index("seq") * tok_rows).astype(jnp.float32)
    positions = offset + jnp.arange(tok_rows, dtype=jnp.float32)
    cosine, sine_table = rotary_tables(positions, KEY)
    key_scale = 1.0 / math.sqrt(KEY)
    query_rotated = rotate(
        query_lin.reshape(seq_count, tok_rows, local_heads, KEY), cosine, sine_table
    ).astype(jnp.bfloat16)
    key_rotated = (
        rotate(key_lin.reshape(seq_count, tok_rows, local_heads, KEY), cosine, sine_table)
        * key_scale
    ).astype(jnp.bfloat16)
    value_matrix_rows = value_lin.reshape(seq_count, tok_rows, local_heads, VAL).astype(
        jnp.bfloat16
    )
    decay_mask, leading_decay, trailing_decay = decay_tables(decay_rate, tok_rows)
    whole_decay = jnp.exp(-decay_rate * tok_rows)[:, None, None]
    summary = jax.vmap(block_summary, in_axes=(0, 0, None))(
        key_rotated, value_matrix_rows, trailing_decay
    )
    incoming_state = carry_states(whole_decay, summary)
    retained = jax.vmap(block_output, in_axes=(0, 0, 0, 0, None, None))(
        query_rotated, key_rotated, value_matrix_rows, incoming_state, decay_mask, leading_decay
    )
    group_normed, group_inv = normalize(retained, EPS_GROUP)
    gate_act, gate_slope = swish_parts(gate_lin)
    group_flat = group_normed.reshape(row_count, local_heads * VAL)
    mixed = (gate_act * group_flat).astype(jnp.bfloat16)
    attn_out = lax.psum(jnp.dot(mixed, full_out, preferred_element_type=jnp.float32), "tp")
    middle = residual + attn_out
    normed_two, inv_two = normalize(middle, EPS_LAYER)
    ffn_in = (normed_two * full_ffn_gain.astype(jnp.float32)).astype(jnp.bfloat16)
    glu_lin = jnp.dot(ffn_in, full_glu, preferred_element_type=jnp.float32)
    up_lin = jnp.dot(ffn_in, full_up, preferred_element_type=jnp.float32)
    glu_act, glu_slope = swish_parts(glu_lin)
    hidden = (glu_act * up_lin).astype(jnp.bfloat16)
    ffn_out = lax.psum(jnp.dot(hidden, full_down, preferred_element_type=jnp.float32), "tp")
    final = middle + ffn_out
    outputs = final.astype(jnp.bfloat16).reshape(seq_count, tok_rows, model_width)
    back_weights = (
        lax.all_gather(w_query, "seq", axis=0, tiled=True),
        lax.all_gather(w_key, "seq", axis=0, tiled=True),
        lax.all_gather(w_value, "seq", axis=0, tiled=True),
        lax.all_gather(w_gate, "seq", axis=0, tiled=True),
        lax.all_gather(w_out, "seq", axis=1, tiled=True),
        lax.all_gather(w_glu, "seq", axis=0, tiled=True),
        lax.all_gather(w_up, "seq", axis=0, tiled=True),
        lax.all_gather(w_down, "seq", axis=1, tiled=True),
        lax.all_gather(attn_gain, "seq", axis=0, tiled=True),
        lax.all_gather(ffn_gain, "seq", axis=0, tiled=True),
    )
    (
        back_query,
        back_key,
        back_value,
        back_gate,
        back_out,
        back_glu,
        back_up,
        back_down,
        back_attn_gain,
        back_ffn_gain,
    ) = back_weights
    cot_rows = cotangent.reshape(row_count, model_width)
    down_grad = jnp.dot(hidden.T, cot_rows, preferred_element_type=jnp.float32)
    grad_hidden = jnp.dot(cot_rows, back_down.T, preferred_element_type=jnp.float32)
    grad_glu = (grad_hidden * up_lin * glu_slope).astype(jnp.bfloat16)
    grad_up = (grad_hidden * glu_act).astype(jnp.bfloat16)
    glu_grad = jnp.dot(ffn_in.T, grad_glu, preferred_element_type=jnp.float32)
    up_grad = jnp.dot(ffn_in.T, grad_up, preferred_element_type=jnp.float32)
    grad_ffn_in = lax.psum(
        jnp.dot(grad_glu, back_glu.T, preferred_element_type=jnp.float32)
        + jnp.dot(grad_up, back_up.T, preferred_element_type=jnp.float32),
        "tp",
    )
    ffngain_grad = jnp.sum(grad_ffn_in * normed_two, axis=0)
    grad_middle = cot_rows.astype(jnp.float32) + normalize_back(
        grad_ffn_in * back_ffn_gain.astype(jnp.float32), normed_two, inv_two
    )
    grad_middle_bf = grad_middle.astype(jnp.bfloat16)
    out_grad = jnp.dot(mixed.T, grad_middle_bf, preferred_element_type=jnp.float32)
    grad_mixed = jnp.dot(grad_middle_bf, back_out.T, preferred_element_type=jnp.float32)
    grad_gate = (grad_mixed * group_flat * gate_slope).astype(jnp.bfloat16)
    grad_group = (grad_mixed * gate_act).reshape(seq_count, tok_rows, local_heads, VAL)
    grad_retained = normalize_back(grad_group, group_normed, group_inv).astype(jnp.bfloat16)
    own_grad = jax.vmap(state_grad_own, in_axes=(0, 0, None))(
        query_rotated, grad_retained, leading_decay
    )
    state_gradient = carry_back(whole_decay, own_grad)
    grad_qrot, grad_krot, grad_vrows = jax.vmap(
        block_backward, in_axes=(0, 0, 0, 0, 0, 0, None, None, None)
    )(
        query_rotated,
        key_rotated,
        value_matrix_rows,
        incoming_state,
        state_gradient,
        grad_retained,
        decay_mask,
        leading_decay,
        trailing_decay,
    )
    query_gradient = (
        rotate_back(grad_qrot, cosine, sine_table)
        .reshape(row_count, local_heads * KEY)
        .astype(jnp.bfloat16)
    )
    key_gradient = (
        (rotate_back(grad_krot, cosine, sine_table) * key_scale)
        .reshape(row_count, local_heads * KEY)
        .astype(jnp.bfloat16)
    )
    value_gradient = grad_vrows.reshape(row_count, local_heads * VAL).astype(jnp.bfloat16)
    query_grad = jnp.dot(attn_in.T, query_gradient, preferred_element_type=jnp.float32)
    key_grad = jnp.dot(attn_in.T, key_gradient, preferred_element_type=jnp.float32)
    value_grad = jnp.dot(attn_in.T, value_gradient, preferred_element_type=jnp.float32)
    gate_grad = jnp.dot(attn_in.T, grad_gate, preferred_element_type=jnp.float32)
    partial_in = (
        jnp.dot(query_gradient, back_query.T, preferred_element_type=jnp.float32)
        + jnp.dot(key_gradient, back_key.T, preferred_element_type=jnp.float32)
        + jnp.dot(value_gradient, back_value.T, preferred_element_type=jnp.float32)
        + jnp.dot(grad_gate, back_gate.T, preferred_element_type=jnp.float32)
    )
    grad_attn_in = lax.psum(partial_in, "tp")
    attngain_grad = jnp.sum(grad_attn_in * normed_one, axis=0)
    input_grad = grad_middle + normalize_back(
        grad_attn_in * back_attn_gain.astype(jnp.float32), normed_one, inv_one
    )
    input_out = input_grad.reshape(seq_count, tok_rows, model_width)
    reduced = (
        lax.psum_scatter(query_grad, "seq", scatter_dimension=0, tiled=True),
        lax.psum_scatter(key_grad, "seq", scatter_dimension=0, tiled=True),
        lax.psum_scatter(value_grad, "seq", scatter_dimension=0, tiled=True),
        lax.psum_scatter(gate_grad, "seq", scatter_dimension=0, tiled=True),
        lax.psum_scatter(out_grad, "seq", scatter_dimension=1, tiled=True),
        lax.psum_scatter(glu_grad, "seq", scatter_dimension=0, tiled=True),
        lax.psum_scatter(up_grad, "seq", scatter_dimension=0, tiled=True),
        lax.psum_scatter(down_grad, "seq", scatter_dimension=1, tiled=True),
        lax.psum_scatter(attngain_grad, "seq", scatter_dimension=0, tiled=True),
        lax.psum_scatter(ffngain_grad, "seq", scatter_dimension=0, tiled=True),
    )
    return (
        outputs,
        input_out,
        reduced[8],
        reduced[0],
        reduced[1],
        reduced[2],
        reduced[3],
        reduced[4],
        reduced[9],
        reduced[5],
        reduced[6],
        reduced[7],
    )


def solution(mesh):
    return jax.shard_map(
        on_device,
        mesh=mesh,
        in_specs=(
            P(None, "seq", None),
            P(None, "seq", None),
            P("seq"),
            P("seq", "tp"),
            P("seq", "tp"),
            P("seq", "tp"),
            P("seq", "tp"),
            P("tp", "seq"),
            P("seq"),
            P("seq", "tp"),
            P("seq", "tp"),
            P("tp", "seq"),
            P("tp"),
        ),
        out_specs=(
            P(None, "seq", None),
            P(None, "seq", None),
            P("seq"),
            P("seq", "tp"),
            P("seq", "tp"),
            P("seq", "tp"),
            P("seq", "tp"),
            P("tp", "seq"),
            P("seq"),
            P("seq", "tp"),
            P("seq", "tp"),
            P("tp", "seq"),
        ),
        check_vma=False,
    )
```

profile of v0, /device:TPU:0, one launch (start us, length us, event | category | flops | bytes accessed | tf_op | source)
XLA Modules:
  0.0 2463.8 jit_solution(17136700813776060130)
XLA Ops:
  10.8 22.4 all-gather
  39.4 22.7 all-gather.17.cloned.1.call-done
  66.0 45.9 %all-gather.15.cloned.1.call-done = bf16[2048,512]{1,0:T(8,128)(2,1)} async-done(((bf16[256,512]{1,0:T(8,128)(2,1)}), bf16[2048,512]{1,0:T(8,128)(2,1)}) %all-gather.15.cloned.1.call-update) | async-done | bytes 2097168 | tf_op jit(solution)/shard_map/all_gather | solution.py:194
  122.3 57.4 %all-gather.13.cloned.1.call-done = bf16[2048,864]{0,1:T(8,128)(2,1)} async-done(((bf16[256,864]{0,1:T(8,128)(2,1)}), bf16[2048,864]{0,1:T(8,128)(2,1)}) %all-gather.13.cloned.1.call-update) | async-done | bytes 3538960 | tf_op jit(solution)/shard_map/all_gather | solution.py:196
  186.6 373.1 %while.20 = (s32[]{:T(128)}, f32[2,2,256,432]{2,3,1,0:T(8,128)S(1)}, f32[2]{0:T(128)S(1)}, f32[2,2,256,432]{2,3,1,0:T(8,128)S(1)}, s32[]{:T(128)}) while((s32[]{:T(128)}, f32[2,2,256,432]{2,3,1,0:T(8,128)S(1)}, f32[2]{0:T(128)S(1)}, f32[2,2,256,432]{2,3,1,0:T(8,128)S(1)}, s32[]{:T(128)}) %tuple.65), condition=%wide.region_3.4_spmd, body=%wide.region_2.3_spmd.sunk | while | flops 884738 | bytes 12386413 | solution.py:164
  191.6 48.9 %collective-permute-done = f32[2,2,256,432]{2,3,1,0:T(8,128)S(1)} collective-permute-done((f32[2,2,256,432]{2,3,1,0:T(8,128)}, f32[2,2,256,432]{2,3,1,0:T(8,128)S(1)}, u32[]{:S(2)}, u32[]{:S(2)}) %collective-permute-start) | collective-permute-done | bytes 1769504 | tf_op jit(solution)/shard_map/while/body/eval_jaxpr/ppermute | solution.py:17
  242.2 23.1 collective-permute-start
  265.2 42.4 %collective-permute-done = f32[2,2,256,432]{2,3,1,0:T(8,128)S(1)} collective-permute-done((f32[2,2,256,432]{2,3,1,0:T(8,128)}, f32[2,2,256,432]{2,3,1,0:T(8,128)S(1)}, u32[]{:S(2)}, u32[]{:S(2)}) %collective-permute-start) | collective-permute-done | bytes 1769504 | tf_op jit(solution)/shard_map/while/body/eval_jaxpr/ppermute | solution.py:17
  309.3 18.4 collective-permute-start
  327.7 50.1 %collective-permute-done = f32[2,2,256,432]{2,3,1,0:T(8,128)S(1)} collective-permute-done((f32[2,2,256,432]{2,3,1,0:T(8,128)}, f32[2,2,256,432]{2,3,1,0:T(8,128)S(1)}, u32[]{:S(2)}, u32[]{:S(2)}) %collective-permute-start) | collective-permute-done | bytes 1769504 | tf_op jit(solution)/shard_map/while/body/eval_jaxpr/ppermute | solution.py:17
  379.3 13.7 collective-permute-start
  393.1 37.7 %collective-permute-done = f32[2,2,256,432]{2,3,1,0:T(8,128)S(1)} collective-permute-done((f32[2,2,256,432]{2,3,1,0:T(8,128)}, f32[2,2,256,432]{2,3,1,0:T(8,128)S(1)}, u32[]{:S(2)}, u32[]{:S(2)}) %collective-permute-start) | collective-permute-done | bytes 1769504 | tf_op jit(solution)/shard_map/while/body/eval_jaxpr/ppermute | solution.py:17
  437.6 36.8 %collective-permute-done = f32[2,2,256,432]{2,3,1,0:T(8,128)S(1)} collective-permute-done((f32[2,2,256,432]{2,3,1,0:T(8,128)}, f32[2,2,256,432]{2,3,1,0:T(8,128)S(1)}, u32[]{:S(2)}, u32[]{:S(2)}) %collective-permute-start) | collective-permute-done | bytes 1769504 | tf_op jit(solution)/shard_map/while/body/eval_jaxpr/ppermute | solution.py:17
  481.3 36.0 %collective-permute-done = f32[2,2,256,432]{2,3,1,0:T(8,128)S(1)} collective-permute-done((f32[2,2,256,432]{2,3,1,0:T(8,128)}, f32[2,2,256,432]{2,3,1,0:T(8,128)S(1)}, u32[]{:S(2)}, u32[]{:S(2)}) %collective-permute-start) | collective-permute-done | bytes 1769504 | tf_op jit(solution)/shard_map/while/body/eval_jaxpr/ppermute | solution.py:17
  524.1 35.1 %collective-permute-done = f32[2,2,256,432]{2,3,1,0:T(8,128)S(1)} collective-permute-done((f32[2,2,256,432]{2,3,1,0:T(8,128)}, f32[2,2,256,432]{2,3,1,0:T(8,128)S(1)}, u32[]{:S(2)}, u32[]{:S(2)}) %collective-permute-start) | collective-permute-done | bytes 1769504 | tf_op jit(solution)/shard_map/while/body/eval_jaxpr/ppermute | solution.py:17
  566.3 6.9 multiply_convert_fusion.6
  573.2 6.7 fusion.64
  582.2 19.7 all-gather.1
  601.9 65.3 %all-reduce.8.cloned.1.call-done = f32[512,2048]{1,0:T(8,128)} async-done(((f32[512,2048]{1,0:T(8,128)}), f32[512,2048]{1,0:T(8,128)}) %all-reduce.8.cloned.1.call-update) | async-done | bytes 4194320 | tf_op jit(solution)/shard_map/psum | solution.py:251
  674.6 62.0 %all-gather.21.cloned.1.call-done = bf16[2048,864]{0,1:T(8,128)(2,1)} async-done(((bf16[256,864]{0,1:T(8,128)(2,1)}), bf16[2048,864]{0,1:T(8,128)(2,1)}) %all-gather.21.cloned.1.call-update) | async-done | bytes 3538960 | tf_op jit(solution)/shard_map/all_gather | solution.py:199
  742.5 61.6 %all-gather.23.cloned.1.call-done = bf16[2048,864]{0,1:T(8,128)(2,1)} async-done(((bf16[256,864]{0,1:T(8,128)(2,1)}), bf16[2048,864]{0,1:T(8,128)(2,1)}) %all-gather.23.cloned.1.call-update) | async-done | bytes 3538960 | tf_op jit(solution)/shard_map/all_gather | solution.py:200
  804.0 5.9 fusion.66
  809.9 61.5 %all-gather.25.cloned.1.call-done = bf16[864,2048]{1,0:T(8,128)(2,1)} async-done(((bf16[864,256]{1,0:T(8,128)(2,1)}), bf16[864,2048]{1,0:T(8,128)(2,1)}) %all-gather.25.cloned.1.call-update) | async-done | bytes 3538960 | tf_op jit(solution)/shard_map/all_gather | solution.py:201
  871.5 7.4 multiply_convert_fusion.3
  886.5 6.6 fusion.67
  893.1 76.8 %all-reduce.10.cloned.1.call-done = f32[512,2048]{1,0:T(8,128)} async-done(((f32[512,2048]{1,0:T(8,128)}), f32[512,2048]{1,0:T(8,128)}) %all-reduce.10.cloned.1.call-update) | async-done | bytes 4194320 | tf_op jit(solution)/shard_map/psum | solution.py:293
  1001.3 293.0 %while.21 = (s32[]{:T(128)}, f32[2,2,256,432]{2,3,1,0:T(8,128)S(1)}, f32[2]{0:T(128)S(1)}, f32[2,2,256,432]{2,3,1,0:T(8,128)S(1)}, s32[]{:T(128)}) while((s32[]{:T(128)}, f32[2,2,256,432]{2,3,1,0:T(8,128)S(1)}, f32[2]{0:T(128)S(1)}, f32[2,2,256,432]{2,3,1,0:T(8,128)S(1)}, s32[]{:T(128)}) %tuple.110), condition=%wide.region_16.17_spmd, body=%wide.region_15.16_spmd.sunk | while | flops 884738 | bytes 12386413 | solution.py:172
  1004.1 40.8 %collective-permute-done.1 = f32[2,2,256,432]{2,3,1,0:T(8,128)S(1)} collective-permute-done((f32[2,2,256,432]{2,3,1,0:T(8,128)}, f32[2,2,256,432]{2,3,1,0:T(8,128)S(1)}, u32[]{:S(2)}, u32[]{:S(2)}) %collective-permute-start.1) | collective-permute-done | bytes 1769504 | tf_op jit(solution)/shard_map/while/body/eval_jaxpr/ppermute | solution.py:17
  1047.8 40.6 %collective-permute-done.1 = f32[2,2,256,432]{2,3,1,0:T(8,128)S(1)} collective-permute-done((f32[2,2,256,432]{2,3,1,0:T(8,128)}, f32[2,2,256,432]{2,3,1,0:T(8,128)S(1)}, u32[]{:S(2)}, u32[]{:S(2)}) %collective-permute-start.1) | collective-permute-done | bytes 1769504 | tf_op jit(solution)/shard_map/while/body/eval_jaxpr/ppermute | solution.py:17
  1091.2 40.0 %collective-permute-done.1 = f32[2,2,256,432]{2,3,1,0:T(8,128)S(1)} collective-permute-done((f32[2,2,256,432]{2,3,1,0:T(8,128)}, f32[2,2,256,432]{2,3,1,0:T(8,128)S(1)}, u32[]{:S(2)}, u32[]{:S(2)}) %collective-permute-start.1) | collective-permute-done | bytes 1769504 | tf_op jit(solution)/shard_map/while/body/eval_jaxpr/ppermute | solution.py:17
  1134.1 39.2 %collective-permute-done.1 = f32[2,2,256,432]{2,3,1,0:T(8,128)S(1)} collective-permute-done((f32[2,2,256,432]{2,3,1,0:T(8,128)}, f32[2,2,256,432]{2,3,1,0:T(8,128)S(1)}, u32[]{:S(2)}, u32[]{:S(2)}) %collective-permute-start.1) | collective-permute-done | bytes 1769504 | tf_op jit(solution)/shard_map/while/body/eval_jaxpr/ppermute | solution.py:17
  1176.1 38.3 %collective-permute-done.1 = f32[2,2,256,432]{2,3,1,0:T(8,128)S(1)} collective-permute-done((f32[2,2,256,432]{2,3,1,0:T(8,128)}, f32[2,2,256,432]{2,3,1,0:T(8,128)S(1)}, u32[]{:S(2)}, u32[]{:S(2)}) %collective-permute-start.1) | collective-permute-done | bytes 1769504 | tf_op jit(solution)/shard_map/while/body/eval_jaxpr/ppermute | solution.py:17
  1217.2 37.5 %collective-permute-done.1 = f32[2,2,256,432]{2,3,1,0:T(8,128)S(1)} collective-permute-done((f32[2,2,256,432]{2,3,1,0:T(8,128)}, f32[2,2,256,432]{2,3,1,0:T(8,128)S(1)}, u32[]{:S(2)}, u32[]{:S(2)}) %collective-permute-start.1) | collective-permute-done | bytes 1769504 | tf_op jit(solution)/shard_map/while/body/eval_jaxpr/ppermute | solution.py:17
  1257.5 36.6 %collective-permute-done.1 = f32[2,2,256,432]{2,3,1,0:T(8,128)S(1)} collective-permute-done((f32[2,2,256,432]{2,3,1,0:T(8,128)}, f32[2,2,256,432]{2,3,1,0:T(8,128)S(1)}, u32[]{:S(2)}, u32[]{:S(2)}) %collective-permute-start.1) | collective-permute-done | bytes 1769504 | tf_op jit(solution)/shard_map/while/body/eval_jaxpr/ppermute | solution.py:17
  1328.2 6.4 fusion.78
  1335.7 6.6 fusion.79
  1343.5 6.6 fusion.75
  1351.2 7.1 fusion.44
  1373.0 101.1 %all-reduce.12.cloned.1.call-done = (f32[512,2048]{1,0:T(8,128)}, f32[512,2048]{1,0:T(8,128)}) async-done(((f32[512,2048]{1,0:T(8,128)}, f32[512,2048]{1,0:T(8,128)}), (f32[512,2048]{1,0:T(8,128)}, f32[512,2048]{1,0:T(8,128)})) %all-reduce.12.cloned.1.call-update) | async-done | bytes 8388624 | tf_op jit(solution)/shard_map/psum | solution.py:259
  1477.6 38.5 %all-reduce.2 = (f32[2048]{0:T(1024)S(1)}, f32[2048]{0:T(1024)S(1)}) all-reduce(f32[2048]{0:T(1024)S(1)} %get-tuple-element.76, f32[2048]{0:T(1024)S(1)} %copy-done.58), channel_id=2, replica_groups=mesh['seq'=8,'tp'=4] {'seq'}, use_global_device_ids=true, to_apply=%region_21.22.clone | all-reduce | flops 4096 | bytes 32768
  1527.2 39.8 %reduce-scatter.11.cloned.1.call-done = f32[256,512]{1,0:T(8,128)} async-done(((f32[2048,512]{1,0:T(8,128)}), f32[256,512]{1,0:T(8,128)}) %reduce-scatter.11.cloned.1.call-update) | async-done | bytes 524304 | tf_op jit(solution)/shard_map/reduce_scatter | solution.py:354
  1567.0 92.2 %reduce-scatter.9.cloned.1.call-done = f32[256,512]{1,0:T(8,128)} async-done(((f32[2048,512]{1,0:T(8,128)}), f32[256,512]{1,0:T(8,128)}) %reduce-scatter.9.cloned.1.call-update) | async-done | bytes 524304 | tf_op jit(solution)/shard_map/reduce_scatter | solution.py:353
  1659.2 133.3 %reduce-scatter.19.cloned.1.call-done = f32[256,864]{0,1:T(8,128)} async-done(((f32[2048,864]{0,1:T(8,128)}), f32[256,864]{0,1:T(8,128)}) %reduce-scatter.19.cloned.1.call-update) | async-done | bytes 884752 | tf_op jit(solution)/shard_map/reduce_scatter | solution.py:358
  1792.5 132.8 %reduce-scatter.21.cloned.1.call-done = f32[256,864]{0,1:T(8,128)} async-done(((f32[2048,864]{0,1:T(8,128)}), f32[256,864]{0,1:T(8,128)}) %reduce-scatter.21.cloned.1.call-update) | async-done | bytes 884752 | tf_op jit(solution)/shard_map/reduce_scatter | solution.py:359
  1925.3 132.8 %reduce-scatter.23.cloned.1.call-done = f32[864,256]{1,0:T(8,128)} async-done(((f32[864,2048]{1,0:T(8,128)}), f32[864,256]{1,0:T(8,128)}) %reduce-scatter.23.cloned.1.call-update) | async-done | bytes 884752 | tf_op jit(solution)/shard_map/reduce_scatter | solution.py:360
  2058.2 132.8 %reduce-scatter.17.cloned.1.call-done = f32[864,256]{1,0:T(8,128)} async-done(((f32[864,2048]{1,0:T(8,128)}), f32[864,256]{1,0:T(8,128)}) %reduce-scatter.17.cloned.1.call-update) | async-done | bytes 884752 | tf_op jit(solution)/shard_map/reduce_scatter | solution.py:357
  2191.0 132.8 %reduce-scatter.13.cloned.1.call-done = f32[256,864]{0,1:T(8,128)} async-done(((f32[2048,864]{0,1:T(8,128)}), f32[256,864]{0,1:T(8,128)}) %reduce-scatter.13.cloned.1.call-update) | async-done | bytes 884752 | tf_op jit(solution)/shard_map/reduce_scatter | solution.py:355
  2323.8 133.0 %reduce-scatter.15.cloned.1.call-done = f32[256,864]{0,1:T(8,128)} async-done(((f32[2048,864]{0,1:T(8,128)}), f32[256,864]{0,1:T(8,128)}) %reduce-scatter.15.cloned.1.call-update) | async-done | bytes 884752 | tf_op jit(solution)/shard_map/reduce_scatter | solution.py:356
  (295 shorter events, 207.3 us)
Async XLA Ops:
  7.2 26.1 %copy-start.2 = (bf16[2,256,2048]{2,1,0:T(8,128)(2,1)S(1)}, bf16[2,256,2048]{2,1,0:T(8,128)(2,1)}, u32[]{:S(2)}) copy-start(bf16[2,256,2048]{2,1,0:T(8,128)(2,1)} %param.17) | copy-start | bytes 6291460
  7.2 54.9 %all-gather.17.cloned.1.call-start = ((), (), s32[]{:S(2)}) async-start(), calls=%async_computation.11 | async-start | bytes 2359296 | tf_op jit(solution)/shard_map/all_gather | solution.py:195
  7.9 103.9 %all-gather.15.cloned.1.call-start = ((), (), s32[]{:S(2)}) async-start(), calls=%async_computation.10 | async-start | bytes 2359296 | tf_op jit(solution)/shard_map/all_gather | solution.py:194
  8.7 171.0 %all-gather.13.cloned.1.call-start = ((), (), s32[]{:S(2)}) async-start(), calls=%async_computation.9 | async-start | bytes 3981312 | tf_op jit(solution)/shard_map/all_gather | solution.py:196
  9.4 556.9 %all-gather.11.cloned.1.call-start = ((), (), s32[]{:S(2)}) async-start(), calls=%async_computation.8 | async-start | bytes 3981312 | tf_op jit(solution)/shard_map/all_gather | solution.py:197
  10.0 563.2 %all-gather.19.cloned.1.call-start = ((), (), s32[]{:S(2)}) async-start(), calls=%async_computation.12 | async-start | bytes 3981312 | tf_op jit(solution)/shard_map/all_gather | solution.py:198
  10.6 656.7 %all-reduce.8.cloned.1.call-start = ((), (), s32[]{:S(2)}) async-start(), calls=%async_computation.13 | async-start | bytes 8388608 | tf_op jit(solution)/shard_map/psum | solution.py:251
  34.9 85.6 %copy-start.39 = (f32[256,256]{0,1:T(8,128)}, f32[256,256]{0,1:T(8,128)S(1)}, u32[]{:S(2)}) copy-start(f32[256,256]{0,1:T(8,128)S(1)} %pad_maximum_fusion) | copy-start | bytes 786436
  35.0 85.6 %copy-start.38 = (f32[256,256]{0,1:T(8,128)}, f32[256,256]{0,1:T(8,128)S(1)}, u32[]{:S(2)}) copy-start(f32[256,256]{0,1:T(8,128)S(1)} %pad_maximum_fusion.1) | copy-start | bytes 786436
  37.2 83.8 %copy-start.30 = (f32[2,256,256]{2,1,0:T(8,128)}, f32[2,256,256]{2,1,0:T(8,128)S(1)}, u32[]{:S(2)}) copy-start(f32[2,256,256]{2,1,0:T(8,128)S(1)} %exponential_select_fusion) | copy-start | bytes 1572868
  37.3 148.1 %copy-start.59 = (f32[256,2]{0,1:T(2,128)}, f32[256,2]{0,1:T(2,128)S(1)}, u32[]{:S(2)}) copy-start(f32[256,2]{0,1:T(2,128)S(1)} %get-tuple-element.128) | copy-start | bytes 6148
  37.3 522.4 %copy-start.61 = (f32[256,2]{0,1:T(2,128)}, f32[256,2]{0,1:T(2,128)S(1)}, u32[]{:S(2)}) copy-start(f32[256,2]{0,1:T(2,128)S(1)} %get-tuple-element.127) | copy-start | bytes 6148
  122.3 61.4 %copy-start.28 = (bf16[2,2,256,256]{3,2,1,0:T(8,128)(2,1)}, bf16[2,2,256,256]{3,2,1,0:T(8,128)(2,1)S(1)}, u32[]{:S(2)}) copy-start(bf16[2,2,256,256]{3,2,1,0:T(8,128)(2,1)S(1)} %fusion.35) | copy-start | bytes 1572868
  188.2 52.4 %collective-permute-start = (f32[2,2,256,432]{2,3,1,0:T(8,128)}, f32[2,2,256,432]{2,3,1,0:T(8,128)S(1)}, u32[]{:S(2)}, u32[]{:S(2)}) collective-permute-start(f32[2,2,256,432]{2,3,1,0:T(8,128)} %multiply_add_fusion.5), channel_id=1, source_target_pairs={{0,4},{4,8},{8,12},{12,16},{16,20},{20,24},{24,28},{1,5},{5,9},{9,... | collective-permute-start | bytes 5308424 | tf_op jit(solution)/shard_map/while/body/eval_jaxpr/ppermute | solution.py:17
  242.2 65.5 %collective-permute-start = (f32[2,2,256,432]{2,3,1,0:T(8,128)}, f32[2,2,256,432]{2,3,1,0:T(8,128)S(1)}, u32[]{:S(2)}, u32[]{:S(2)}) collective-permute-start(f32[2,2,256,432]{2,3,1,0:T(8,128)} %multiply_add_fusion.5), channel_id=1, source_target_pairs={{0,4},{4,8},{8,12},{12,16},{16,20},{20,24},{24,28},{1,5},{5,9},{9,... | collective-permute-start | bytes 5308424 | tf_op jit(solution)/shard_map/while/body/eval_jaxpr/ppermute | solution.py:17
  309.3 68.5 %collective-permute-start = (f32[2,2,256,432]{2,3,1,0:T(8,128)}, f32[2,2,256,432]{2,3,1,0:T(8,128)S(1)}, u32[]{:S(2)}, u32[]{:S(2)}) collective-permute-start(f32[2,2,256,432]{2,3,1,0:T(8,128)} %multiply_add_fusion.5), channel_id=1, source_target_pairs={{0,4},{4,8},{8,12},{12,16},{16,20},{20,24},{24,28},{1,5},{5,9},{9,... | collective-permute-start | bytes 5308424 | tf_op jit(solution)/shard_map/while/body/eval_jaxpr/ppermute | solution.py:17
  379.3 51.4 %collective-permute-start = (f32[2,2,256,432]{2,3,1,0:T(8,128)}, f32[2,2,256,432]{2,3,1,0:T(8,128)S(1)}, u32[]{:S(2)}, u32[]{:S(2)}) collective-permute-start(f32[2,2,256,432]{2,3,1,0:T(8,128)} %multiply_add_fusion.5), channel_id=1, source_target_pairs={{0,4},{4,8},{8,12},{12,16},{16,20},{20,24},{24,28},{1,5},{5,9},{9,... | collective-permute-start | bytes 5308424 | tf_op jit(solution)/shard_map/while/body/eval_jaxpr/ppermute | solution.py:17
  432.3 42.1 %collective-permute-start = (f32[2,2,256,432]{2,3,1,0:T(8,128)}, f32[2,2,256,432]{2,3,1,0:T(8,128)S(1)}, u32[]{:S(2)}, u32[]{:S(2)}) collective-permute-start(f32[2,2,256,432]{2,3,1,0:T(8,128)} %multiply_add_fusion.5), channel_id=1, source_target_pairs={{0,4},{4,8},{8,12},{12,16},{16,20},{20,24},{24,28},{1,5},{5,9},{9,... | collective-permute-start | bytes 5308424 | tf_op jit(solution)/shard_map/while/body/eval_jaxpr/ppermute | solution.py:17
  476.0 41.2 %collective-permute-start = (f32[2,2,256,432]{2,3,1,0:T(8,128)}, f32[2,2,256,432]{2,3,1,0:T(8,128)S(1)}, u32[]{:S(2)}, u32[]{:S(2)}) collective-permute-start(f32[2,2,256,432]{2,3,1,0:T(8,128)} %multiply_add_fusion.5), channel_id=1, source_target_pairs={{0,4},{4,8},{8,12},{12,16},{16,20},{20,24},{24,28},{1,5},{5,9},{9,... | collective-permute-start | bytes 5308424 | tf_op jit(solution)/shard_map/while/body/eval_jaxpr/ppermute | solution.py:17
  518.8 40.4 %collective-permute-start = (f32[2,2,256,432]{2,3,1,0:T(8,128)}, f32[2,2,256,432]{2,3,1,0:T(8,128)S(1)}, u32[]{:S(2)}, u32[]{:S(2)}) collective-permute-start(f32[2,2,256,432]{2,3,1,0:T(8,128)} %multiply_add_fusion.5), channel_id=1, source_target_pairs={{0,4},{4,8},{8,12},{12,16},{16,20},{20,24},{24,28},{1,5},{5,9},{9,... | collective-permute-start | bytes 5308424 | tf_op jit(solution)/shard_map/while/body/eval_jaxpr/ppermute | solution.py:17
  579.9 156.7 %all-gather.21.cloned.1.call-start = ((), (), s32[]{:S(2)}) async-start(), calls=%async_computation.14 | async-start | bytes 3981312 | tf_op jit(solution)/shard_map/all_gather | solution.py:199
  580.6 223.4 %all-gather.23.cloned.1.call-start = ((), (), s32[]{:S(2)}) async-start(), calls=%async_computation.15 | async-start | bytes 3981312 | tf_op jit(solution)/shard_map/all_gather | solution.py:200
  581.4 290.1 %all-gather.25.cloned.1.call-start = ((), (), s32[]{:S(2)}) async-start(), calls=%async_computation.16 | async-start | bytes 3981312 | tf_op jit(solution)/shard_map/all_gather | solution.py:201
  582.1 387.7 %all-reduce.10.cloned.1.call-start = ((), (), s32[]{:S(2)}) async-start(), calls=%async_computation.17 | async-start | bytes 8388608 | tf_op jit(solution)/shard_map/psum | solution.py:293
  871.5 7.4 copy-start.21
  886.0 588.0 %all-reduce.12.cloned.1.call-start = ((), (), s32[]{:S(2)}) async-start(), calls=%async_computation.26 | async-start | bytes 16777216 | tf_op jit(solution)/shard_map/psum | solution.py:259
  969.9 6.0 copy-start.57
  1001.3 293.0 %copy-start.60 = (f32[256,2]{0,1:T(2,128)S(1)}, f32[256,2]{0,1:T(2,128)}, u32[]{:S(2)}) copy-start(f32[256,2]{0,1:T(2,128)} %copy-done.59) | copy-start | bytes 6148
  1002.8 42.1 %collective-permute-start.1 = (f32[2,2,256,432]{2,3,1,0:T(8,128)}, f32[2,2,256,432]{2,3,1,0:T(8,128)S(1)}, u32[]{:S(2)}, u32[]{:S(2)}) collective-permute-start(f32[2,2,256,432]{2,3,1,0:T(8,128)} %multiply_add_fusion.6), channel_id=1, source_target_pairs={{4,0},{8,4},{12,8},{16,12},{20,16},{24,20},{28,24},{5,1},{9,5},{13... | collective-permute-start | bytes 5308424 | tf_op jit(solution)/shard_map/while/body/eval_jaxpr/ppermute | solution.py:17
  1046.5 41.9 %collective-permute-start.1 = (f32[2,2,256,432]{2,3,1,0:T(8,128)}, f32[2,2,256,432]{2,3,1,0:T(8,128)S(1)}, u32[]{:S(2)}, u32[]{:S(2)}) collective-permute-start(f32[2,2,256,432]{2,3,1,0:T(8,128)} %multiply_add_fusion.6), channel_id=1, source_target_pairs={{4,0},{8,4},{12,8},{16,12},{20,16},{24,20},{28,24},{5,1},{9,5},{13... | collective-permute-start | bytes 5308424 | tf_op jit(solution)/shard_map/while/body/eval_jaxpr/ppermute | solution.py:17
  1089.9 41.3 %collective-permute-start.1 = (f32[2,2,256,432]{2,3,1,0:T(8,128)}, f32[2,2,256,432]{2,3,1,0:T(8,128)S(1)}, u32[]{:S(2)}, u32[]{:S(2)}) collective-permute-start(f32[2,2,256,432]{2,3,1,0:T(8,128)} %multiply_add_fusion.6), channel_id=1, source_target_pairs={{4,0},{8,4},{12,8},{16,12},{20,16},{24,20},{28,24},{5,1},{9,5},{13... | collective-permute-start | bytes 5308424 | tf_op jit(solution)/shard_map/while/body/eval_jaxpr/ppermute | solution.py:17
  1132.8 40.5 %collective-permute-start.1 = (f32[2,2,256,432]{2,3,1,0:T(8,128)}, f32[2,2,256,432]{2,3,1,0:T(8,128)S(1)}, u32[]{:S(2)}, u32[]{:S(2)}) collective-permute-start(f32[2,2,256,432]{2,3,1,0:T(8,128)} %multiply_add_fusion.6), channel_id=1, source_target_pairs={{4,0},{8,4},{12,8},{16,12},{20,16},{24,20},{28,24},{5,1},{9,5},{13... | collective-permute-start | bytes 5308424 | tf_op jit(solution)/shard_map/while/body/eval_jaxpr/ppermute | solution.py:17
  1174.8 39.6 %collective-permute-start.1 = (f32[2,2,256,432]{2,3,1,0:T(8,128)}, f32[2,2,256,432]{2,3,1,0:T(8,128)S(1)}, u32[]{:S(2)}, u32[]{:S(2)}) collective-permute-start(f32[2,2,256,432]{2,3,1,0:T(8,128)} %multiply_add_fusion.6), channel_id=1, source_target_pairs={{4,0},{8,4},{12,8},{16,12},{20,16},{24,20},{28,24},{5,1},{9,5},{13... | collective-permute-start | bytes 5308424 | tf_op jit(solution)/shard_map/while/body/eval_jaxpr/ppermute | solution.py:17
  1216.0 38.7 %collective-permute-start.1 = (f32[2,2,256,432]{2,3,1,0:T(8,128)}, f32[2,2,256,432]{2,3,1,0:T(8,128)S(1)}, u32[]{:S(2)}, u32[]{:S(2)}) collective-permute-start(f32[2,2,256,432]{2,3,1,0:T(8,128)} %multiply_add_fusion.6), channel_id=1, source_target_pairs={{4,0},{8,4},{12,8},{16,12},{20,16},{24,20},{28,24},{5,1},{9,5},{13... | collective-permute-start | bytes 5308424 | tf_op jit(solution)/shard_map/while/body/eval_jaxpr/ppermute | solution.py:17
  1256.3 37.9 %collective-permute-start.1 = (f32[2,2,256,432]{2,3,1,0:T(8,128)}, f32[2,2,256,432]{2,3,1,0:T(8,128)S(1)}, u32[]{:S(2)}, u32[]{:S(2)}) collective-permute-start(f32[2,2,256,432]{2,3,1,0:T(8,128)} %multiply_add_fusion.6), channel_id=1, source_target_pairs={{4,0},{8,4},{12,8},{16,12},{20,16},{24,20},{28,24},{5,1},{9,5},{13... | collective-permute-start | bytes 5308424 | tf_op jit(solution)/shard_map/while/body/eval_jaxpr/ppermute | solution.py:17
  1318.6 248.4 %reduce-scatter.11.cloned.1.call-start = ((), (), s32[]{:S(2)}) async-start(), calls=%async_computation.19 | async-start | bytes 4718592 | tf_op jit(solution)/shard_map/reduce_scatter | solution.py:354
  1323.5 335.7 %reduce-scatter.9.cloned.1.call-start = ((), (), s32[]{:S(2)}) async-start(), calls=%async_computation.18 | async-start | bytes 4718592 | tf_op jit(solution)/shard_map/reduce_scatter | solution.py:353
  1327.0 465.5 %reduce-scatter.19.cloned.1.call-start = ((), (), s32[]{:S(2)}) async-start(), calls=%async_computation.23 | async-start | bytes 7962624 | tf_op jit(solution)/shard_map/reduce_scatter | solution.py:358
  1334.6 590.7 %reduce-scatter.21.cloned.1.call-start = ((), (), s32[]{:S(2)}) async-start(), calls=%async_computation.24 | async-start | bytes 7962624 | tf_op jit(solution)/shard_map/reduce_scatter | solution.py:359
  1342.3 715.8 %reduce-scatter.23.cloned.1.call-start = ((), (), s32[]{:S(2)}) async-start(), calls=%async_computation.25 | async-start | bytes 7962624 | tf_op jit(solution)/shard_map/reduce_scatter | solution.py:360
  1350.1 840.9 %reduce-scatter.17.cloned.1.call-start = ((), (), s32[]{:S(2)}) async-start(), calls=%async_computation.22 | async-start | bytes 7962624 | tf_op jit(solution)/shard_map/reduce_scatter | solution.py:357
  1358.3 965.6 %reduce-scatter.13.cloned.1.call-start = ((), (), s32[]{:S(2)}) async-start(), calls=%async_computation.20 | async-start | bytes 7962624 | tf_op jit(solution)/shard_map/reduce_scatter | solution.py:355
  1364.4 1092.5 %reduce-scatter.15.cloned.1.call-start = ((), (), s32[]{:S(2)}) async-start(), calls=%async_computation.21 | async-start | bytes 7962624 | tf_op jit(solution)/shard_map/reduce_scatter | solution.py:356
  1371.1 102.9 %copy-start.3 = (bf16[2,256,2048]{2,1,0:T(8,128)(2,1)S(1)}, bf16[2,256,2048]{2,1,0:T(8,128)(2,1)}, u32[]{:S(2)}) copy-start(bf16[2,256,2048]{2,1,0:T(8,128)(2,1)} %param.17) | copy-start | bytes 6291460
  1371.1 102.9 %copy-start.47 = (f32[8,1,256]{2,1,0:T(1,128)S(1)}, f32[8,1,256]{2,1,0:T(1,128)}, u32[]{:S(2)}) copy-start(f32[8,1,256]{2,1,0:T(1,128)} %copy-done.46) | copy-start | bytes 24580
  1371.1 102.9 %copy-start.53 = (f32[1,2,2,128]{3,1,2,0:T(2,128)S(1)}, f32[1,2,2,128]{3,1,2,0:T(2,128)}, u32[]{:S(2)}) copy-start(f32[1,2,2,128]{3,1,2,0:T(2,128)} %copy-done.52) | copy-start | bytes 6148
  1371.1 102.9 %copy-start.55 = (f32[1,2,2,128]{3,1,2,0:T(2,128)S(1)}, f32[1,2,2,128]{3,1,2,0:T(2,128)}, u32[]{:S(2)}) copy-start(f32[1,2,2,128]{3,1,2,0:T(2,128)} %copy-done.54) | copy-start | bytes 6148
  1517.3 6.9 copy-start.9
  (53 other events, 130.1 us)
Sparse Core Ops, SparseCore 0:
  10.1 51.9 all-gather.16
  64.2 47.6 all-gather.14
  113.9 65.6 all-gather.12
  181.6 92.4 all-gather.10
  276.0 88.9 all-gather.18
  580.0 87.2 all-reduce.7
  669.3 67.2 all-gather.20
  738.7 65.3 all-gather.22
  806.1 65.3 all-gather.24
  886.2 83.6 all-reduce.9
  1318.7 155.3 all-reduce.11
  1478.1 88.8 reduce-scatter.10
  1571.2 87.9 reduce-scatter.8
  1663.3 129.1 reduce-scatter.18
  1796.6 128.6 reduce-scatter.20
  1929.5 128.6 reduce-scatter.22
  2062.3 128.6 reduce-scatter.16
  2195.1 128.6 reduce-scatter.12
  2328.1 128.6 reduce-scatter.14
where the time goes:
time: 2470 us; the launch traced here: 2460 us
  waiting for transfers between devices  2050 us (83%)
  matrix products  132 us (5%)
  starting transfers between devices  85.1 us (3%)
  blocking collectives  80.6 us (3%)
  other arithmetic  62.5 us (3%)
  local copies, waits for them, and re-layouts  37.7 us (2%)
    ppermute x14, waiting for transfers between devices, passed_along(): return lax.ppermute(block, axis, route)  560 us
    reduce_scatter x1, waiting for transfers between devices, on_device(): lax.psum_scatter(glu_grad, 'seq', scatter_dimension=0, tiled=True)  133 us
    reduce_scatter x1, waiting for transfers between devices, on_device(): lax.psum_scatter(gate_grad, 'seq', scatter_dimension=0, tiled=True)  133 us
    reduce_scatter x1, waiting for transfers between devices, on_device(): lax.psum_scatter(value_grad, 'seq', scatter_dimension=0, tiled=True)  133 us
    reduce_scatter x1, waiting for transfers between devices, on_device(): lax.psum_scatter(down_grad, 'seq', scatter_dimension=1, tiled=True)  133 us
    reduce_scatter x1, waiting for transfers between devices, on_device(): lax.psum_scatter(out_grad, 'seq', scatter_dimension=1, tiled=True)  133 us
    reduce_scatter x1, waiting for transfers between devices, on_device(): lax.psum_scatter(up_grad, 'seq', scatter_dimension=0, tiled=True)  133 us
    psum x1, waiting for transfers between devices, on_device(): lax.psum(jnp.dot(hidden, full_down, preferred_element_type=jnp.float32),...  101 us
  transfers between devices with their start and end apart: 33, of which 31 were waited for; matrix products, arithmetic and copies ran while one was open for 5% of the time, Pallas kernels for 0%

commit v1 on v0

--- a/solution.py
+++ b/solution.py
@@ -9,6 +9,19 @@
 EPS_LAYER = 1e-05
 EPS_GROUP = 1e-06
 MAXIMAL_ACCURACY = lax.Precision.HIGHEST
+
+
+def _lead_routes_all(a0):
+    item_now, local_part = (jax.lax.psum(1, axis_name="seq"), jax.lax.axis_index("seq"))
+    state_now, answer = (a0, 1)
+    while answer < item_now:
+        state_next = tuple(((w, w ^ answer) for w in range(item_now)))
+        v_now = jax.lax.ppermute(state_now, axis_name="seq", perm=state_next)
+        p_next = jnp.concatenate([state_now, v_now], axis=0)
+        tile_out = jnp.concatenate([v_now, state_now], axis=0)
+        state_now = jnp.where(local_part & answer == 0, p_next, tile_out)
+        answer = 2 * answer
+    return state_now
 
 
 def passed_along(block, axis, distance):
@@ -193,7 +206,7 @@
     gathered = (
         lax.all_gather(w_query, "seq", axis=0, tiled=True),
         lax.all_gather(w_key, "seq", axis=0, tiled=True),
-        lax.all_gather(w_value, "seq", axis=0, tiled=True),
+        _lead_routes_all(w_value),
         lax.all_gather(w_gate, "seq", axis=0, tiled=True),
         lax.all_gather(w_out, "seq", axis=1, tiled=True),
         lax.all_gather(w_glu, "seq", axis=0, tiled=True),

time: 2470 us -> 2500 us (1.012)
    ppermute x0 -> x3, waiting for transfers between devices: none -> 112 us  [_lead_routes_all(): v_now = jax.lax.ppermute(state_now, axis_name='seq', perm=state_next)]
    all_gather x1, waiting for transfers between devices: 57.4 us -> 0.01 us  [on_device(): lax.all_gather(w_value, 'seq', axis=0, tiled=True)]
    all_gather x1, waiting for transfers between devices: 45.9 us -> 13.8 us  [on_device(): lax.all_gather(w_query, 'seq', axis=0, tiled=True)]
  transfers between devices with their start and end apart: 33 -> 36, of which waited for: 31 -> 31; matrix products, arithmetic and copies ran while one was open for 5% -> 8% of each run, Pallas kernels for 0% -> 0%
where the time goes in v1:
time: 2500 us
  waiting for transfers between devices  2060 us (82%)
  matrix products  138 us (6%)
  starting transfers between devices  91.9 us (4%)
  blocking collectives  85.4 us (3%)
  other arithmetic  65.4 us (3%)
  local copies, waits for them, and re-layouts  41.3 us (2%)
    ppermute x14, waiting for transfers between devices, passed_along(): return lax.ppermute(block, axis, route)  574 us
    reduce_scatter x1, waiting for transfers between devices, on_device(): lax.psum_scatter(glu_grad, 'seq', scatter_dimension=0, tiled=True)  133 us
    reduce_scatter x1, waiting for transfers between devices, on_device(): lax.psum_scatter(gate_grad, 'seq', scatter_dimension=0, tiled=True)  133 us
    reduce_scatter x1, waiting for transfers between devices, on_device(): lax.psum_scatter(out_grad, 'seq', scatter_dimension=1, tiled=True)  133 us
    reduce_scatter x1, waiting for transfers between devices, on_device(): lax.psum_scatter(value_grad, 'seq', scatter_dimension=0, tiled=True)  133 us
    reduce_scatter x1, waiting for transfers between devices, on_device(): lax.psum_scatter(down_grad, 'seq', scatter_dimension=1, tiled=True)  133 us
    reduce_scatter x1, waiting for transfers between devices, on_device(): lax.psum_scatter(up_grad, 'seq', scatter_dimension=0, tiled=True)  133 us
    ppermute x3, waiting for transfers between devices, _lead_routes_all(): v_now = jax.lax.ppermute(state_now, axis_name='seq', perm=state_next)  112 us
  transfers between devices with their start and end apart: 36, of which 31 were waited for; matrix products, arithmetic and copies ran while one was open for 8% of the time, Pallas kernels for 0%

profile of v1, /device:TPU:0, one launch (start us, length us, event | category | flops | bytes accessed | tf_op | source)
XLA Modules:
  0.0 2497.9 jit_solution(6314869416019960635)
XLA Ops:
  13.2 25.5 %all-gather = bf16[8,1,256]{2,1,0:T(2,128)(2,1)S(1)} all-gather(bf16[1,1,256]{2,1,0:T(2,128)(2,1)S(1)} %reshape.349), channel_id=1, replica_groups=mesh['seq'=8,'tp'=4] {'seq'}, dimensions={0}, use_global_device_ids=true | all-gather | bytes 4608 | tf_op jit(solution)/shard_map/all_gather | solution.py:215
  43.4 31.6 %collective-permute-done.3 = bf16[512,864]{0,1:T(8,128)(2,1)S(1)} collective-permute-done((bf16[512,864]{0,1:T(8,128)(2,1)S(1)}, bf16[512,864]{0,1:T(8,128)(2,1)S(1)}, u32[]{:S(2)}, u32[]{:S(2)}) %collective-permute-start.3) | collective-permute-done | bytes 884768 | tf_op jit(solution)/shard_map/ppermute | solution.py:19
  78.7 80.1 %collective-permute-done.4 = bf16[1024,864]{0,1:T(8,128)(2,1)S(1)} collective-permute-done((bf16[1024,864]{0,1:T(8,128)(2,1)S(1)}, bf16[1024,864]{0,1:T(8,128)(2,1)S(1)}, u32[]{:S(2)}, u32[]{:S(2)}) %collective-permute-start.4) | collective-permute-done | bytes 1769504 | tf_op jit(solution)/shard_map/ppermute | solution.py:19
  170.7 13.8 all-gather.13.cloned.1.call-done
  197.2 358.0 %while.20 = (s32[]{:T(128)}, f32[2,2,256,432]{2,3,1,0:T(8,128)S(1)}, f32[2]{0:T(128)S(1)}, f32[2,2,256,432]{2,3,1,0:T(8,128)S(1)}, s32[]{:T(128)}) while((s32[]{:T(128)}, f32[2,2,256,432]{2,3,1,0:T(8,128)S(1)}, f32[2]{0:T(128)S(1)}, f32[2,2,256,432]{2,3,1,0:T(8,128)S(1)}, s32[]{:T(128)}) %tuple.66), condition=%wide.region_3.4_spmd, body=%wide.region_2.3_spmd.sunk | while | flops 884738 | bytes 12386413 | solution.py:177
  201.3 52.9 %collective-permute-done = f32[2,2,256,432]{2,3,1,0:T(8,128)S(1)} collective-permute-done((f32[2,2,256,432]{2,3,1,0:T(8,128)}, f32[2,2,256,432]{2,3,1,0:T(8,128)S(1)}, u32[]{:S(2)}, u32[]{:S(2)}) %collective-permute-start) | collective-permute-done | bytes 1769504 | tf_op jit(solution)/shard_map/while/body/eval_jaxpr/ppermute | solution.py:30
  255.7 21.2 collective-permute-start
  276.9 40.6 %collective-permute-done = f32[2,2,256,432]{2,3,1,0:T(8,128)S(1)} collective-permute-done((f32[2,2,256,432]{2,3,1,0:T(8,128)}, f32[2,2,256,432]{2,3,1,0:T(8,128)S(1)}, u32[]{:S(2)}, u32[]{:S(2)}) %collective-permute-start) | collective-permute-done | bytes 1769504 | tf_op jit(solution)/shard_map/while/body/eval_jaxpr/ppermute | solution.py:30
  319.1 22.1 collective-permute-start
  341.1 41.1 %collective-permute-done = f32[2,2,256,432]{2,3,1,0:T(8,128)S(1)} collective-permute-done((f32[2,2,256,432]{2,3,1,0:T(8,128)}, f32[2,2,256,432]{2,3,1,0:T(8,128)S(1)}, u32[]{:S(2)}, u32[]{:S(2)}) %collective-permute-start) | collective-permute-done | bytes 1769504 | tf_op jit(solution)/shard_map/while/body/eval_jaxpr/ppermute | solution.py:30
  383.8 16.4 collective-permute-start
  400.2 34.8 %collective-permute-done = f32[2,2,256,432]{2,3,1,0:T(8,128)S(1)} collective-permute-done((f32[2,2,256,432]{2,3,1,0:T(8,128)}, f32[2,2,256,432]{2,3,1,0:T(8,128)S(1)}, u32[]{:S(2)}, u32[]{:S(2)}) %collective-permute-start) | collective-permute-done | bytes 1769504 | tf_op jit(solution)/shard_map/while/body/eval_jaxpr/ppermute | solution.py:30
  441.8 33.9 %collective-permute-done = f32[2,2,256,432]{2,3,1,0:T(8,128)S(1)} collective-permute-done((f32[2,2,256,432]{2,3,1,0:T(8,128)}, f32[2,2,256,432]{2,3,1,0:T(8,128)S(1)}, u32[]{:S(2)}, u32[]{:S(2)}) %collective-permute-start) | collective-permute-done | bytes 1769504 | tf_op jit(solution)/shard_map/while/body/eval_jaxpr/ppermute | solution.py:30
  482.6 33.1 %collective-permute-done = f32[2,2,256,432]{2,3,1,0:T(8,128)S(1)} collective-permute-done((f32[2,2,256,432]{2,3,1,0:T(8,128)}, f32[2,2,256,432]{2,3,1,0:T(8,128)S(1)}, u32[]{:S(2)}, u32[]{:S(2)}) %collective-permute-start) | collective-permute-done | bytes 1769504 | tf_op jit(solution)/shard_map/while/body/eval_jaxpr/ppermute | solution.py:30
  522.5 32.2 %collective-permute-done = f32[2,2,256,432]{2,3,1,0:T(8,128)S(1)} collective-permute-done((f32[2,2,256,432]{2,3,1,0:T(8,128)}, f32[2,2,256,432]{2,3,1,0:T(8,128)S(1)}, u32[]{:S(2)}, u32[]{:S(2)}) %collective-permute-start) | collective-permute-done | bytes 1769504 | tf_op jit(solution)/shard_map/while/body/eval_jaxpr/ppermute | solution.py:30
  561.9 6.9 multiply_convert_fusion.6
  568.7 6.7 fusion.64
  577.5 21.5 all-gather.1
  599.0 65.1 %all-reduce.8.cloned.1.call-done = f32[512,2048]{1,0:T(8,128)} async-done(((f32[512,2048]{1,0:T(8,128)}), f32[512,2048]{1,0:T(8,128)}) %all-reduce.8.cloned.1.call-update) | async-done | bytes 4194320 | tf_op jit(solution)/shard_map/psum | solution.py:264
  671.5 61.9 %all-gather.19.cloned.1.call-done = bf16[2048,864]{0,1:T(8,128)(2,1)} async-done(((bf16[256,864]{0,1:T(8,128)(2,1)}), bf16[2048,864]{0,1:T(8,128)(2,1)}) %all-gather.19.cloned.1.call-update) | async-done | bytes 3538960 | tf_op jit(solution)/shard_map/all_gather | solution.py:212
  739.2 61.5 %all-gather.21.cloned.1.call-done = bf16[2048,864]{0,1:T(8,128)(2,1)} async-done(((bf16[256,864]{0,1:T(8,128)(2,1)}), bf16[2048,864]{0,1:T(8,128)(2,1)}) %all-gather.21.cloned.1.call-update) | async-done | bytes 3538960 | tf_op jit(solution)/shard_map/all_gather | solution.py:213
  800.8 5.9 fusion.66
  806.7 61.5 %all-gather.23.cloned.1.call-done = bf16[864,2048]{1,0:T(8,128)(2,1)} async-done(((bf16[864,256]{1,0:T(8,128)(2,1)}), bf16[864,2048]{1,0:T(8,128)(2,1)}) %all-gather.23.cloned.1.call-update) | async-done | bytes 3538960 | tf_op jit(solution)/shard_map/all_gather | solution.py:214
  868.2 7.4 multiply_convert_fusion.3
  883.8 6.6 fusion.67
  890.4 76.2 %all-reduce.10.cloned.1.call-done = f32[512,2048]{1,0:T(8,128)} async-done(((f32[512,2048]{1,0:T(8,128)}), f32[512,2048]{1,0:T(8,128)}) %all-reduce.10.cloned.1.call-update) | async-done | bytes 4194320 | tf_op jit(solution)/shard_map/psum | solution.py:306
  996.8 325.5 %while.21 = (s32[]{:T(128)}, f32[2,2,256,432]{2,3,1,0:T(8,128)S(1)}, f32[2]{0:T(128)S(1)}, f32[2,2,256,432]{2,3,1,0:T(8,128)S(1)}, s32[]{:T(128)}) while((s32[]{:T(128)}, f32[2,2,256,432]{2,3,1,0:T(8,128)S(1)}, f32[2]{0:T(128)S(1)}, f32[2,2,256,432]{2,3,1,0:T(8,128)S(1)}, s32[]{:T(128)}) %tuple.111), condition=%wide.region_16.17_spmd, body=%wide.region_15.16_spmd.sunk | while | flops 884738 | bytes 12386413 | solution.py:185
  999.6 59.7 %collective-permute-done.1 = f32[2,2,256,432]{2,3,1,0:T(8,128)S(1)} collective-permute-done((f32[2,2,256,432]{2,3,1,0:T(8,128)}, f32[2,2,256,432]{2,3,1,0:T(8,128)S(1)}, u32[]{:S(2)}, u32[]{:S(2)}) %collective-permute-start.1) | collective-permute-done | bytes 1769504 | tf_op jit(solution)/shard_map/while/body/eval_jaxpr/ppermute | solution.py:30
  1062.1 50.8 %collective-permute-done.1 = f32[2,2,256,432]{2,3,1,0:T(8,128)S(1)} collective-permute-done((f32[2,2,256,432]{2,3,1,0:T(8,128)}, f32[2,2,256,432]{2,3,1,0:T(8,128)S(1)}, u32[]{:S(2)}, u32[]{:S(2)}) %collective-permute-start.1) | collective-permute-done | bytes 1769504 | tf_op jit(solution)/shard_map/while/body/eval_jaxpr/ppermute | solution.py:30
  1115.8 40.7 %collective-permute-done.1 = f32[2,2,256,432]{2,3,1,0:T(8,128)S(1)} collective-permute-done((f32[2,2,256,432]{2,3,1,0:T(8,128)}, f32[2,2,256,432]{2,3,1,0:T(8,128)S(1)}, u32[]{:S(2)}, u32[]{:S(2)}) %collective-permute-start.1) | collective-permute-done | bytes 1769504 | tf_op jit(solution)/shard_map/while/body/eval_jaxpr/ppermute | solution.py:30
  1159.3 39.9 %collective-permute-done.1 = f32[2,2,256,432]{2,3,1,0:T(8,128)S(1)} collective-permute-done((f32[2,2,256,432]{2,3,1,0:T(8,128)}, f32[2,2,256,432]{2,3,1,0:T(8,128)S(1)}, u32[]{:S(2)}, u32[]{:S(2)}) %collective-permute-start.1) | collective-permute-done | bytes 1769504 | tf_op jit(solution)/shard_map/while/body/eval_jaxpr/ppermute | solution.py:30
  1202.0 39.0 %collective-permute-done.1 = f32[2,2,256,432]{2,3,1,0:T(8,128)S(1)} collective-permute-done((f32[2,2,256,432]{2,3,1,0:T(8,128)}, f32[2,2,256,432]{2,3,1,0:T(8,128)S(1)}, u32[]{:S(2)}, u32[]{:S(2)}) %collective-permute-start.1) | collective-permute-done | bytes 1769504 | tf_op jit(solution)/shard_map/while/body/eval_jaxpr/ppermute | solution.py:30
  1243.9 38.2 %collective-permute-done.1 = f32[2,2,256,432]{2,3,1,0:T(8,128)S(1)} collective-permute-done((f32[2,2,256,432]{2,3,1,0:T(8,128)}, f32[2,2,256,432]{2,3,1,0:T(8,128)S(1)}, u32[]{:S(2)}, u32[]{:S(2)}) %collective-permute-start.1) | collective-permute-done | bytes 1769504 | tf_op jit(solution)/shard_map/while/body/eval_jaxpr/ppermute | solution.py:30
  1284.9 37.3 %collective-permute-done.1 = f32[2,2,256,432]{2,3,1,0:T(8,128)S(1)} collective-permute-done((f32[2,2,256,432]{2,3,1,0:T(8,128)}, f32[2,2,256,432]{2,3,1,0:T(8,128)S(1)}, u32[]{:S(2)}, u32[]{:S(2)}) %collective-permute-start.1) | collective-permute-done | bytes 1769504 | tf_op jit(solution)/shard_map/while/body/eval_jaxpr/ppermute | solution.py:30
  1364.8 6.4 fusion.78
  1372.4 6.5 fusion.79
  1380.1 6.5 fusion.75
  1387.7 7.1 fusion.44
  1409.7 98.8 %all-reduce.12.cloned.1.call-done = (f32[512,2048]{1,0:T(8,128)}, f32[512,2048]{1,0:T(8,128)}) async-done(((f32[512,2048]{1,0:T(8,128)}, f32[512,2048]{1,0:T(8,128)}), (f32[512,2048]{1,0:T(8,128)}, f32[512,2048]{1,0:T(8,128)})) %all-reduce.12.cloned.1.call-update) | async-done | bytes 8388624 | tf_op jit(solution)/shard_map/psum | solution.py:272
  1512.0 38.5 %all-reduce.2 = (f32[2048]{0:T(1024)S(1)}, f32[2048]{0:T(1024)S(1)}) all-reduce(f32[2048]{0:T(1024)S(1)} %get-tuple-element.76, f32[2048]{0:T(1024)S(1)} %copy-done.62), channel_id=2, replica_groups=mesh['seq'=8,'tp'=4] {'seq'}, use_global_device_ids=true, to_apply=%region_21.22.clone | all-reduce | flops 4096 | bytes 32768
  1561.6 39.8 %reduce-scatter.11.cloned.1.call-done = f32[256,512]{1,0:T(8,128)} async-done(((f32[2048,512]{1,0:T(8,128)}), f32[256,512]{1,0:T(8,128)}) %reduce-scatter.11.cloned.1.call-update) | async-done | bytes 524304 | tf_op jit(solution)/shard_map/reduce_scatter | solution.py:367
  1601.4 92.2 %reduce-scatter.9.cloned.1.call-done = f32[256,512]{1,0:T(8,128)} async-done(((f32[2048,512]{1,0:T(8,128)}), f32[256,512]{1,0:T(8,128)}) %reduce-scatter.9.cloned.1.call-update) | async-done | bytes 524304 | tf_op jit(solution)/shard_map/reduce_scatter | solution.py:366
  1693.6 133.3 %reduce-scatter.19.cloned.1.call-done = f32[256,864]{0,1:T(8,128)} async-done(((f32[2048,864]{0,1:T(8,128)}), f32[256,864]{0,1:T(8,128)}) %reduce-scatter.19.cloned.1.call-update) | async-done | bytes 884752 | tf_op jit(solution)/shard_map/reduce_scatter | solution.py:371
  1826.9 132.8 %reduce-scatter.21.cloned.1.call-done = f32[256,864]{0,1:T(8,128)} async-done(((f32[2048,864]{0,1:T(8,128)}), f32[256,864]{0,1:T(8,128)}) %reduce-scatter.21.cloned.1.call-update) | async-done | bytes 884752 | tf_op jit(solution)/shard_map/reduce_scatter | solution.py:372
  1959.7 132.8 %reduce-scatter.23.cloned.1.call-done = f32[864,256]{1,0:T(8,128)} async-done(((f32[864,2048]{1,0:T(8,128)}), f32[864,256]{1,0:T(8,128)}) %reduce-scatter.23.cloned.1.call-update) | async-done | bytes 884752 | tf_op jit(solution)/shard_map/reduce_scatter | solution.py:373
  2092.5 132.8 %reduce-scatter.17.cloned.1.call-done = f32[864,256]{1,0:T(8,128)} async-done(((f32[864,2048]{1,0:T(8,128)}), f32[864,256]{1,0:T(8,128)}) %reduce-scatter.17.cloned.1.call-update) | async-done | bytes 884752 | tf_op jit(solution)/shard_map/reduce_scatter | solution.py:370
  2225.4 132.8 %reduce-scatter.13.cloned.1.call-done = f32[256,864]{0,1:T(8,128)} async-done(((f32[2048,864]{0,1:T(8,128)}), f32[256,864]{0,1:T(8,128)}) %reduce-scatter.13.cloned.1.call-update) | async-done | bytes 884752 | tf_op jit(solution)/shard_map/reduce_scatter | solution.py:368
  2358.2 133.0 %reduce-scatter.15.cloned.1.call-done = f32[256,864]{0,1:T(8,128)} async-done(((f32[2048,864]{0,1:T(8,128)}), f32[256,864]{0,1:T(8,128)}) %reduce-scatter.15.cloned.1.call-update) | async-done | bytes 884752 | tf_op jit(solution)/shard_map/reduce_scatter | solution.py:369
  (309 shorter events, 221.8 us)
Async XLA Ops:
  7.2 155.3 %all-gather.15.cloned.1.call-start = ((), (), s32[]{:S(2)}) async-start(), calls=%async_computation.10 | async-start | bytes 2359296 | tf_op jit(solution)/shard_map/all_gather | solution.py:208
  7.9 176.5 %all-gather.13.cloned.1.call-start = ((), (), s32[]{:S(2)}) async-start(), calls=%async_computation.9 | async-start | bytes 2359296 | tf_op jit(solution)/shard_map/all_gather | solution.py:207
  8.7 553.2 %all-gather.11.cloned.1.call-start = ((), (), s32[]{:S(2)}) async-start(), calls=%async_computation.8 | async-start | bytes 3981312 | tf_op jit(solution)/shard_map/all_gather | solution.py:210
  9.4 559.3 %all-gather.17.cloned.1.call-start = ((), (), s32[]{:S(2)}) async-start(), calls=%async_computation.11 | async-start | bytes 3981312 | tf_op jit(solution)/shard_map/all_gather | solution.py:211
  9.5 32.1 %collective-permute-start.2 = (bf16[256,864]{0,1:T(8,128)(2,1)}, bf16[256,864]{0,1:T(8,128)(2,1)S(1)}, u32[]{:S(2)}, u32[]{:S(2)}) collective-permute-start(bf16[256,864]{0,1:T(8,128)(2,1)} %param.22), channel_id=1, source_target_pairs={{0,4},{4,0},{8,12},{12,8},{16,20},{20,16},{24,28},{28,24},{1,5},{5... | collective-permute-start | bytes 1327112 | tf_op jit(solution)/shard_map/ppermute | solution.py:19
  12.5 651.6 %all-reduce.8.cloned.1.call-start = ((), (), s32[]{:S(2)}) async-start(), calls=%async_computation.12 | async-start | bytes 8388608 | tf_op jit(solution)/shard_map/psum | solution.py:264
  38.7 37.9 %copy-start.50 = (f32[8,1,256]{2,1,0:T(1,128)}, f32[8,1,256]{2,1,0:T(1,128)S(1)}, u32[]{:S(2)}) copy-start(f32[8,1,256]{2,1,0:T(1,128)S(1)} %convert_element_type.136) | copy-start | bytes 24580
  41.5 35.2 %copy-start.56 = (f32[1,2,2,128]{3,1,2,0:T(2,128)}, f32[1,2,2,128]{3,1,2,0:T(2,128)S(1)}, u32[]{:S(2)}) copy-start(f32[1,2,2,128]{3,1,2,0:T(2,128)S(1)} %copy.103) | copy-start | bytes 6148
  41.5 35.2 %copy-start.58 = (f32[1,2,2,128]{3,1,2,0:T(2,128)}, f32[1,2,2,128]{3,1,2,0:T(2,128)S(1)}, u32[]{:S(2)}) copy-start(f32[1,2,2,128]{3,1,2,0:T(2,128)S(1)} %copy.102) | copy-start | bytes 6148
  41.7 33.3 %collective-permute-start.3 = (bf16[512,864]{0,1:T(8,128)(2,1)S(1)}, bf16[512,864]{0,1:T(8,128)(2,1)S(1)}, u32[]{:S(2)}, u32[]{:S(2)}) collective-permute-start(bf16[512,864]{0,1:T(8,128)(2,1)S(1)} %maximum_select_fusion.2), channel_id=1, source_target_pairs={{0,8},{4,12},{8,0},{12,4},{16,24},{20,28},{24,16},{28,20},{1,9},{5... | collective-permute-start | bytes 2654216 | tf_op jit(solution)/shard_map/ppermute | solution.py:19
  75.6 83.3 %collective-permute-start.4 = (bf16[1024,864]{0,1:T(8,128)(2,1)S(1)}, bf16[1024,864]{0,1:T(8,128)(2,1)S(1)}, u32[]{:S(2)}, u32[]{:S(2)}) collective-permute-start(bf16[1024,864]{0,1:T(8,128)(2,1)S(1)} %maximum_select_fusion.1), channel_id=1, source_target_pairs={{0,16},{4,20},{8,24},{12,28},{16,0},{20,4},{24,8},{28,12},{1,17},{... | collective-permute-start | bytes 5308424 | tf_op jit(solution)/shard_map/ppermute | solution.py:19
  75.7 119.1 %copy-start.63 = (f32[256,2]{0,1:T(2,128)}, f32[256,2]{0,1:T(2,128)S(1)}, u32[]{:S(2)}) copy-start(f32[256,2]{0,1:T(2,128)S(1)} %get-tuple-element.128) | copy-start | bytes 6148
  75.8 479.5 %copy-start.65 = (f32[256,2]{0,1:T(2,128)}, f32[256,2]{0,1:T(2,128)S(1)}, u32[]{:S(2)}) copy-start(f32[256,2]{0,1:T(2,128)S(1)} %get-tuple-element.127) | copy-start | bytes 6148
  75.9 116.9 %copy-start.33 = (f32[2,256,256]{2,1,0:T(8,128)}, f32[2,256,256]{2,1,0:T(8,128)S(1)}, u32[]{:S(2)}) copy-start(f32[2,256,256]{2,1,0:T(8,128)S(1)} %exponential_select_fusion) | copy-start | bytes 1572868
  76.6 83.8 %copy-start.7 = (bf16[2,256,2048]{2,1,0:T(8,128)(2,1)}, bf16[2,256,2048]{2,1,0:T(8,128)(2,1)S(1)}, u32[]{:S(2)}) copy-start(bf16[2,256,2048]{2,1,0:T(8,128)(2,1)S(1)} %fusion.4) | copy-start | bytes 6291460
  198.7 55.5 %collective-permute-start = (f32[2,2,256,432]{2,3,1,0:T(8,128)}, f32[2,2,256,432]{2,3,1,0:T(8,128)S(1)}, u32[]{:S(2)}, u32[]{:S(2)}) collective-permute-start(f32[2,2,256,432]{2,3,1,0:T(8,128)} %multiply_add_fusion.5), channel_id=1, source_target_pairs={{0,4},{4,8},{8,12},{12,16},{16,20},{20,24},{24,28},{1,5},{5,9},{9,... | collective-permute-start | bytes 5308424 | tf_op jit(solution)/shard_map/while/body/eval_jaxpr/ppermute | solution.py:30
  255.7 61.9 %collective-permute-start = (f32[2,2,256,432]{2,3,1,0:T(8,128)}, f32[2,2,256,432]{2,3,1,0:T(8,128)S(1)}, u32[]{:S(2)}, u32[]{:S(2)}) collective-permute-start(f32[2,2,256,432]{2,3,1,0:T(8,128)} %multiply_add_fusion.5), channel_id=1, source_target_pairs={{0,4},{4,8},{8,12},{12,16},{16,20},{20,24},{24,28},{1,5},{5,9},{9,... | collective-permute-start | bytes 5308424 | tf_op jit(solution)/shard_map/while/body/eval_jaxpr/ppermute | solution.py:30
  319.1 63.2 %collective-permute-start = (f32[2,2,256,432]{2,3,1,0:T(8,128)}, f32[2,2,256,432]{2,3,1,0:T(8,128)S(1)}, u32[]{:S(2)}, u32[]{:S(2)}) collective-permute-start(f32[2,2,256,432]{2,3,1,0:T(8,128)} %multiply_add_fusion.5), channel_id=1, source_target_pairs={{0,4},{4,8},{8,12},{12,16},{16,20},{20,24},{24,28},{1,5},{5,9},{9,... | collective-permute-start | bytes 5308424 | tf_op jit(solution)/shard_map/while/body/eval_jaxpr/ppermute | solution.py:30
  383.8 51.2 %collective-permute-start = (f32[2,2,256,432]{2,3,1,0:T(8,128)}, f32[2,2,256,432]{2,3,1,0:T(8,128)S(1)}, u32[]{:S(2)}, u32[]{:S(2)}) collective-permute-start(f32[2,2,256,432]{2,3,1,0:T(8,128)} %multiply_add_fusion.5), channel_id=1, source_target_pairs={{0,4},{4,8},{8,12},{12,16},{16,20},{20,24},{24,28},{1,5},{5,9},{9,... | collective-permute-start | bytes 5308424 | tf_op jit(solution)/shard_map/while/body/eval_jaxpr/ppermute | solution.py:30
  436.5 39.2 %collective-permute-start = (f32[2,2,256,432]{2,3,1,0:T(8,128)}, f32[2,2,256,432]{2,3,1,0:T(8,128)S(1)}, u32[]{:S(2)}, u32[]{:S(2)}) collective-permute-start(f32[2,2,256,432]{2,3,1,0:T(8,128)} %multiply_add_fusion.5), channel_id=1, source_target_pairs={{0,4},{4,8},{8,12},{12,16},{16,20},{20,24},{24,28},{1,5},{5,9},{9,... | collective-permute-start | bytes 5308424 | tf_op jit(solution)/shard_map/while/body/eval_jaxpr/ppermute | solution.py:30
  477.3 38.4 %collective-permute-start = (f32[2,2,256,432]{2,3,1,0:T(8,128)}, f32[2,2,256,432]{2,3,1,0:T(8,128)S(1)}, u32[]{:S(2)}, u32[]{:S(2)}) collective-permute-start(f32[2,2,256,432]{2,3,1,0:T(8,128)} %multiply_add_fusion.5), channel_id=1, source_target_pairs={{0,4},{4,8},{8,12},{12,16},{16,20},{20,24},{24,28},{1,5},{5,9},{9,... | collective-permute-start | bytes 5308424 | tf_op jit(solution)/shard_map/while/body/eval_jaxpr/ppermute | solution.py:30
  517.2 37.5 %collective-permute-start = (f32[2,2,256,432]{2,3,1,0:T(8,128)}, f32[2,2,256,432]{2,3,1,0:T(8,128)S(1)}, u32[]{:S(2)}, u32[]{:S(2)}) collective-permute-start(f32[2,2,256,432]{2,3,1,0:T(8,128)} %multiply_add_fusion.5), channel_id=1, source_target_pairs={{0,4},{4,8},{8,12},{12,16},{16,20},{20,24},{24,28},{1,5},{5,9},{9,... | collective-permute-start | bytes 5308424 | tf_op jit(solution)/shard_map/while/body/eval_jaxpr/ppermute | solution.py:30
  575.4 158.0 %all-gather.19.cloned.1.call-start = ((), (), s32[]{:S(2)}) async-start(), calls=%async_computation.13 | async-start | bytes 3981312 | tf_op jit(solution)/shard_map/all_gather | solution.py:212
  576.0 224.8 %all-gather.21.cloned.1.call-start = ((), (), s32[]{:S(2)}) async-start(), calls=%async_computation.14 | async-start | bytes 3981312 | tf_op jit(solution)/shard_map/all_gather | solution.py:213
  576.7 291.5 %all-gather.23.cloned.1.call-start = ((), (), s32[]{:S(2)}) async-start(), calls=%async_computation.15 | async-start | bytes 3981312 | tf_op jit(solution)/shard_map/all_gather | solution.py:214
  577.5 389.1 %all-reduce.10.cloned.1.call-start = ((), (), s32[]{:S(2)}) async-start(), calls=%async_computation.16 | async-start | bytes 8388608 | tf_op jit(solution)/shard_map/psum | solution.py:306
  882.8 463.9 %all-gather.25.cloned.1.call-start = ((), (), s32[]{:S(2)}) async-start(), calls=%async_computation.17 | async-start | bytes 3981312 | tf_op jit(solution)/shard_map/all_gather | solution.py:278
  883.4 625.2 %all-reduce.12.cloned.1.call-start = ((), (), s32[]{:S(2)}) async-start(), calls=%async_computation.26 | async-start | bytes 16777216 | tf_op jit(solution)/shard_map/psum | solution.py:272
  996.8 325.6 %copy-start.64 = (f32[256,2]{0,1:T(2,128)S(1)}, f32[256,2]{0,1:T(2,128)}, u32[]{:S(2)}) copy-start(f32[256,2]{0,1:T(2,128)} %copy-done.63) | copy-start | bytes 6148
  998.3 61.0 %collective-permute-start.1 = (f32[2,2,256,432]{2,3,1,0:T(8,128)}, f32[2,2,256,432]{2,3,1,0:T(8,128)S(1)}, u32[]{:S(2)}, u32[]{:S(2)}) collective-permute-start(f32[2,2,256,432]{2,3,1,0:T(8,128)} %multiply_add_fusion.6), channel_id=1, source_target_pairs={{4,0},{8,4},{12,8},{16,12},{20,16},{24,20},{28,24},{5,1},{9,5},{13... | collective-permute-start | bytes 5308424 | tf_op jit(solution)/shard_map/while/body/eval_jaxpr/ppermute | solution.py:30
  1060.8 52.1 %collective-permute-start.1 = (f32[2,2,256,432]{2,3,1,0:T(8,128)}, f32[2,2,256,432]{2,3,1,0:T(8,128)S(1)}, u32[]{:S(2)}, u32[]{:S(2)}) collective-permute-start(f32[2,2,256,432]{2,3,1,0:T(8,128)} %multiply_add_fusion.6), channel_id=1, source_target_pairs={{4,0},{8,4},{12,8},{16,12},{20,16},{24,20},{28,24},{5,1},{9,5},{13... | collective-permute-start | bytes 5308424 | tf_op jit(solution)/shard_map/while/body/eval_jaxpr/ppermute | solution.py:30
  1114.5 42.0 %collective-permute-start.1 = (f32[2,2,256,432]{2,3,1,0:T(8,128)}, f32[2,2,256,432]{2,3,1,0:T(8,128)S(1)}, u32[]{:S(2)}, u32[]{:S(2)}) collective-permute-start(f32[2,2,256,432]{2,3,1,0:T(8,128)} %multiply_add_fusion.6), channel_id=1, source_target_pairs={{4,0},{8,4},{12,8},{16,12},{20,16},{24,20},{28,24},{5,1},{9,5},{13... | collective-permute-start | bytes 5308424 | tf_op jit(solution)/shard_map/while/body/eval_jaxpr/ppermute | solution.py:30
  1158.0 41.2 %collective-permute-start.1 = (f32[2,2,256,432]{2,3,1,0:T(8,128)}, f32[2,2,256,432]{2,3,1,0:T(8,128)S(1)}, u32[]{:S(2)}, u32[]{:S(2)}) collective-permute-start(f32[2,2,256,432]{2,3,1,0:T(8,128)} %multiply_add_fusion.6), channel_id=1, source_target_pairs={{4,0},{8,4},{12,8},{16,12},{20,16},{24,20},{28,24},{5,1},{9,5},{13... | collective-permute-start | bytes 5308424 | tf_op jit(solution)/shard_map/while/body/eval_jaxpr/ppermute | solution.py:30
  1200.7 40.3 %collective-permute-start.1 = (f32[2,2,256,432]{2,3,1,0:T(8,128)}, f32[2,2,256,432]{2,3,1,0:T(8,128)S(1)}, u32[]{:S(2)}, u32[]{:S(2)}) collective-permute-start(f32[2,2,256,432]{2,3,1,0:T(8,128)} %multiply_add_fusion.6), channel_id=1, source_target_pairs={{4,0},{8,4},{12,8},{16,12},{20,16},{24,20},{28,24},{5,1},{9,5},{13... | collective-permute-start | bytes 5308424 | tf_op jit(solution)/shard_map/while/body/eval_jaxpr/ppermute | solution.py:30
  1242.6 39.5 %collective-permute-start.1 = (f32[2,2,256,432]{2,3,1,0:T(8,128)}, f32[2,2,256,432]{2,3,1,0:T(8,128)S(1)}, u32[]{:S(2)}, u32[]{:S(2)}) collective-permute-start(f32[2,2,256,432]{2,3,1,0:T(8,128)} %multiply_add_fusion.6), channel_id=1, source_target_pairs={{4,0},{8,4},{12,8},{16,12},{20,16},{24,20},{28,24},{5,1},{9,5},{13... | collective-permute-start | bytes 5308424 | tf_op jit(solution)/shard_map/while/body/eval_jaxpr/ppermute | solution.py:30
  1283.6 38.6 %collective-permute-start.1 = (f32[2,2,256,432]{2,3,1,0:T(8,128)}, f32[2,2,256,432]{2,3,1,0:T(8,128)S(1)}, u32[]{:S(2)}, u32[]{:S(2)}) collective-permute-start(f32[2,2,256,432]{2,3,1,0:T(8,128)} %multiply_add_fusion.6), channel_id=1, source_target_pairs={{4,0},{8,4},{12,8},{16,12},{20,16},{24,20},{28,24},{5,1},{9,5},{13... | collective-permute-start | bytes 5308424 | tf_op jit(solution)/shard_map/while/body/eval_jaxpr/ppermute | solution.py:30
  1355.3 246.1 %reduce-scatter.11.cloned.1.call-start = ((), (), s32[]{:S(2)}) async-start(), calls=%async_computation.19 | async-start | bytes 4718592 | tf_op jit(solution)/shard_map/reduce_scatter | solution.py:367
  1360.2 333.4 %reduce-scatter.9.cloned.1.call-start = ((), (), s32[]{:S(2)}) async-start(), calls=%async_computation.18 | async-start | bytes 4718592 | tf_op jit(solution)/shard_map/reduce_scatter | solution.py:366
  1363.7 463.3 %reduce-scatter.19.cloned.1.call-start = ((), (), s32[]{:S(2)}) async-start(), calls=%async_computation.23 | async-start | bytes 7962624 | tf_op jit(solution)/shard_map/reduce_scatter | solution.py:371
  1371.2 588.5 %reduce-scatter.21.cloned.1.call-start = ((), (), s32[]{:S(2)}) async-start(), calls=%async_computation.24 | async-start | bytes 7962624 | tf_op jit(solution)/shard_map/reduce_scatter | solution.py:372
  1378.9 713.6 %reduce-scatter.23.cloned.1.call-start = ((), (), s32[]{:S(2)}) async-start(), calls=%async_computation.25 | async-start | bytes 7962624 | tf_op jit(solution)/shard_map/reduce_scatter | solution.py:373
  1386.6 838.8 %reduce-scatter.17.cloned.1.call-start = ((), (), s32[]{:S(2)}) async-start(), calls=%async_computation.22 | async-start | bytes 7962624 | tf_op jit(solution)/shard_map/reduce_scatter | solution.py:370
  1394.8 963.4 %reduce-scatter.13.cloned.1.call-start = ((), (), s32[]{:S(2)}) async-start(), calls=%async_computation.20 | async-start | bytes 7962624 | tf_op jit(solution)/shard_map/reduce_scatter | solution.py:368
  1401.1 1090.1 %reduce-scatter.15.cloned.1.call-start = ((), (), s32[]{:S(2)}) async-start(), calls=%async_computation.21 | async-start | bytes 7962624 | tf_op jit(solution)/shard_map/reduce_scatter | solution.py:369
  1407.8 100.7 %copy-start.3 = (bf16[2,256,2048]{2,1,0:T(8,128)(2,1)S(1)}, bf16[2,256,2048]{2,1,0:T(8,128)(2,1)}, u32[]{:S(2)}) copy-start(bf16[2,256,2048]{2,1,0:T(8,128)(2,1)} %param.17) | copy-start | bytes 6291460
  1407.8 100.7 %copy-start.51 = (f32[8,1,256]{2,1,0:T(1,128)S(1)}, f32[8,1,256]{2,1,0:T(1,128)}, u32[]{:S(2)}) copy-start(f32[8,1,256]{2,1,0:T(1,128)} %copy-done.50) | copy-start | bytes 24580
  1407.8 100.7 %copy-start.57 = (f32[1,2,2,128]{3,1,2,0:T(2,128)S(1)}, f32[1,2,2,128]{3,1,2,0:T(2,128)}, u32[]{:S(2)}) copy-start(f32[1,2,2,128]{3,1,2,0:T(2,128)} %copy-done.56) | copy-start | bytes 6148
  1407.9 100.7 %copy-start.59 = (f32[1,2,2,128]{3,1,2,0:T(2,128)S(1)}, f32[1,2,2,128]{3,1,2,0:T(2,128)}, u32[]{:S(2)}) copy-start(f32[1,2,2,128]{3,1,2,0:T(2,128)} %copy-done.58) | copy-start | bytes 6148
  (59 other events, 273.8 us)
Sparse Core Ops, SparseCore 0:
  10.1 60.8 all-gather.14
  73.2 111.2 all-gather.12
  186.5 88.5 all-gather.10
  277.0 94.9 all-gather.16
  575.5 88.5 all-reduce.7
  666.0 67.2 all-gather.18
  735.4 65.3 all-gather.20
  802.8 65.3 all-gather.22
  882.9 83.6 all-reduce.9
  968.5 91.6 all-gather.24
  1355.4 153.0 all-reduce.11
  1512.6 88.8 reduce-scatter.10
  1605.6 87.9 reduce-scatter.8
  1697.7 129.1 reduce-scatter.18
  1831.1 128.6 reduce-scatter.20
  1963.9 128.6 reduce-scatter.22
  2096.7 128.6 reduce-scatter.16
  2229.5 128.6 reduce-scatter.12
  2362.5 128.6 reduce-scatter.14
